TPU v7x, 128 devices: a whole 4x4x4 slice. The times are simulated.
128 devices in a mesh: fsdp: 32 (over x_hi, z, y), tensor: 4 (over x_lo, core).
Axes of the slice: x: 4 (x_hi: 2, x_lo: 2; x = x_hi * 2 + x_lo), y: 4, z: 4, core: 2. Of those that a mesh axis runs over, the one named last changes fastest.
Arguments:
- activations: bfloat16 [32768, 5120], P('fsdp', 'tensor'), may hold values from -6 to 6
- cotangent: bfloat16 [32768, 5120], P('fsdp', 'tensor'), may hold values from -0.032958984 to 0.032958984
- weights: float32 [5120, 5120], P(None, ('tensor', 'fsdp')), may hold values from -0.025 to 0.025
- first_moment: float32 [5120, 5120], P(None, ('tensor', 'fsdp')), may hold values from -3 to 3
- second_moment: float32 [5120, 5120], P(None, ('tensor', 'fsdp')), may hold values from 0.01 to 1
Outputs:
- weights_new: float32 [5120, 5120], P('fsdp', 'tensor')
- first_new: float32 [5120, 5120], P('fsdp', 'tensor')
- second_new: float32 [5120, 5120], P('fsdp', 'tensor')
- weights_bf16: bfloat16 [5120, 5120], P(None, 'tensor')
All inputs are finite; a program needn't handle non-finite values.
Results may differ from a plain program's by a relative error of at most 0.014.
Values may be sent and summed in bfloat16 or wider, within the bound.
No kernel may reach another device: no remote copies, remote signals or barrier semaphores. Data moves between devices by JAX's collectives and lax.ppermute only.
A program may use at most 128 MiB of HBM per device.

v0:
```python
import jax
import jax.numpy as jnp
from jax import lax
from jax.sharding import PartitionSpec as P

STEP = 20
beta_one = 0.9
beta_two = 0.95
adam_eps = 1e-08
learn_rate = 0.0003
decay_rate = 0.1


def split_up(value, dim, count):
    before, after = (value.shape[:dim], value.shape[dim + 1 :])
    return jnp.moveaxis(value.reshape(*before, count, -1, *after), dim, 0)


def sent_and_summed(value, axis, dim):
    count = lax.axis_size(axis)
    parts = lax.all_to_all(split_up(value, dim, count), axis, 0, 0, tiled=True)
    return jnp.sum(parts.astype(jnp.float32), axis=0)


def adam_update(weights, first_moment, second_moment, gradient):
    first_new = beta_one * first_moment + (1.0 - beta_one) * gradient
    second_new = beta_two * second_moment + (1.0 - beta_two) * gradient * gradient
    corrected = first_new / (1.0 - beta_one**STEP)
    scaled = jnp.sqrt(second_new / (1.0 - beta_two**STEP)) + adam_eps
    weights_new = weights - learn_rate * (corrected / scaled + decay_rate * weights)
    return (weights_new, first_new, second_new)


def body(activations, cotangent, weights, first_moment, second_moment):
    gathered = lax.all_gather(activations, "tensor", axis=1, tiled=True)
    transposed = sent_and_summed(
        lax.dot_general(
            cotangent, gathered, (((0,), (0,)), ((), ())), preferred_element_type=jnp.float32
        ).astype(jnp.bfloat16),
        "fsdp",
        0,
    )
    gradient = transposed.T
    weights_old, first_old, second_old = adam_update(weights, first_moment, second_moment, gradient)
    weights_bf16 = lax.all_gather(weights_old.astype(jnp.bfloat16), "fsdp", axis=1, tiled=True)
    weights_new, first_new, second_new = (
        lax.all_to_all(
            weights_old.astype(jnp.bfloat16), "fsdp", split_axis=0, concat_axis=1, tiled=True
        ).astype(weights_old.dtype),
        lax.all_to_all(
            first_old.astype(jnp.bfloat16), "fsdp", split_axis=0, concat_axis=1, tiled=True
        ).astype(first_old.dtype),
        lax.all_to_all(
            second_old.astype(jnp.bfloat16), "fsdp", split_axis=0, concat_axis=1, tiled=True
        ).astype(second_old.dtype),
    )
    return (weights_new, first_new, second_new, weights_bf16)


def solution(mesh):
    return jax.shard_map(
        body,
        mesh=mesh,
        in_specs=(
            P("fsdp", "tensor"),
            P("fsdp", "tensor"),
            P(None, ("tensor", "fsdp")),
            P(None, ("tensor", "fsdp")),
            P(None, ("tensor", "fsdp")),
        ),
        out_specs=(
            P("fsdp", "tensor"),
            P("fsdp", "tensor"),
            P("fsdp", "tensor"),
            P(None, "tensor"),
        ),
        check_vma=False,
    )
```

profile of v0, /device:TPU:0, one launch (start us, length us, event | category | flops | bytes accessed | tf_op | source)
XLA Modules:
  0.0 469.7 jit_solution(9544911949169199346)
XLA Ops:
  7.2 0.7 all-gather.3.cloned.1.call-update
  8.0 101.3 %all-gather.3.cloned.1.call-done = bf16[1024,5120]{1,0:T(8,128)(2,1)} async-done(((bf16[1024,1280]{1,0:T(8,128)(2,1)}), bf16[1024,5120]{1,0:T(8,128)(2,1)}) %all-gather.3.cloned.1.call-update) | async-done | bytes 10485776 | tf_op jit(solution)/shard_map/all_gather | solution.py:35
  109.3 20.2 %convolution_convert_fusion = bf16[1280,5120]{1,0:T(8,128)(2,1)} fusion(bf16[1024,1280]{1,0:T(8,128)(2,1)S(1)} %copy-done, bf16[1024,5120]{1,0:T(8,128)(2,1)} %all-gather.3.cloned.1.call-done), kind=kOutput, calls=%fused_computation.1 | convolution fusion | flops 13428326400 | bytes 26214400 | tf_op jit(solution)/shard_map/dot_general | solution.py:37
  129.5 158.0 %all_to_all.44 = bf16[32,40,5120]{2,1,0:T(8,128)(2,1)} all-to-all(bf16[32,40,5120]{2,1,0:T(8,128)(2,1)} %bitcast.31), channel_id=1, replica_groups=mesh['fsdp'=32,'tensor'=4] {'fsdp'}, dimensions={0} | all-to-all | bytes 26214400 | tf_op jit(solution)/shard_map/all_to_all | solution.py:21
  287.4 7.7 %convert_reduce_fusion = f32[40,5120]{1,0:T(8,128)S(1)} fusion(bf16[32,40,5120]{2,1,0:T(8,128)(2,1)} %all_to_all.44), kind=kLoop, calls=%fused_computation | loop fusion | flops 12902400 | bytes 13926400 | tf_op jit(solution)/shard_map/reduce_sum | solution.py:22
  295.1 2.6 fusion.3
  297.7 0.8 all_to_all.38
  298.5 1.2 copy.28
  299.7 7.0 %all-to-all-start.3 = ((bf16[32,160,40]{1,2,0:T(8,128)(2,1)}), bf16[32,160,40]{1,2,0:T(8,128)(2,1)S(1)}, u32[]{:S(2)}, u32[]{:S(2)}) async-start(bf16[32,160,40]{1,2,0:T(8,128)(2,1)} %copy.28), calls=%async_computation.3 | async-start | bytes 1310720 | tf_op jit(solution)/shard_map/all_to_all | solution.py:53
  306.8 0.8 all_to_all.36
  307.6 1.2 copy.27
  308.8 13.6 %all-to-all-done.3 = bf16[32,160,40]{1,2,0:T(8,128)(2,1)S(1)} async-done(((bf16[32,160,40]{1,2,0:T(8,128)(2,1)}), bf16[32,160,40]{1,2,0:T(8,128)(2,1)S(1)}, u32[]{:S(2)}, u32[]{:S(2)}) %all-to-all-start.3) | async-done | bytes 409632 | tf_op jit(solution)/shard_map/all_to_all | solution.py:53
  322.4 4.7 %all-to-all-start.2 = ((bf16[32,160,40]{1,2,0:T(8,128)(2,1)}), bf16[32,160,40]{1,2,0:T(8,128)(2,1)S(1)}, u32[]{:S(2)}, u32[]{:S(2)}) async-start(bf16[32,160,40]{1,2,0:T(8,128)(2,1)} %copy.27), calls=%async_computation.2 | async-start | bytes 1310720 | tf_op jit(solution)/shard_map/all_to_all | solution.py:50
  327.1 1.8 all_to_all.34
  328.9 1.2 copy.26
  330.1 10.4 %all-to-all-done.2 = bf16[32,160,40]{1,2,0:T(8,128)(2,1)S(1)} async-done(((bf16[32,160,40]{1,2,0:T(8,128)(2,1)}), bf16[32,160,40]{1,2,0:T(8,128)(2,1)S(1)}, u32[]{:S(2)}, u32[]{:S(2)}) %all-to-all-start.2) | async-done | bytes 409632 | tf_op jit(solution)/shard_map/all_to_all | solution.py:50
  340.5 4.0 all-to-all-start.1
  344.6 1.3 copy.31
  346.0 1.3 copy.30
  347.2 16.4 %all-to-all-done.1 = bf16[32,160,40]{1,2,0:T(8,128)(2,1)S(1)} async-done(((bf16[32,160,40]{1,2,0:T(8,128)(2,1)}), bf16[32,160,40]{1,2,0:T(8,128)(2,1)S(1)}, u32[]{:S(2)}, u32[]{:S(2)}) %all-to-all-start.1) | async-done | bytes 409632 | tf_op jit(solution)/shard_map/all_to_all | solution.py:47
  363.6 1.2 convert_element_type.60
  364.8 2.7 copy.29
  367.5 77.8 %all-gather.5.cloned.1.call-done = bf16[5120,1280]{0,1:T(8,128)(2,1)} async-done(((bf16[5120,40]{0,1:T(8,128)(2,1)}), bf16[5120,1280]{0,1:T(8,128)(2,1)}) %all-gather.5.cloned.1.call-update) | async-done | bytes 13107216 | tf_op jit(solution)/shard_map/all_gather | solution.py:45
  445.3 17.6 %copy.32 = bf16[5120,1280]{1,0:T(8,128)(2,1)} copy(bf16[5120,1280]{0,1:T(8,128)(2,1)} %all-gather.5.cloned.1.call-done) | data formatting | bytes 26214400
  (13 shorter events, 0.3 us)
Async XLA Ops:
  7.2 102.1 %copy-start = (bf16[1024,1280]{1,0:T(8,128)(2,1)S(1)}, bf16[1024,1280]{1,0:T(8,128)(2,1)}, u32[]{:S(2)}) copy-start(bf16[1024,1280]{1,0:T(8,128)(2,1)} %param.6) | copy-start | bytes 7864324
  7.2 102.1 %all-gather.3.cloned.1.call-start = ((), (), s32[]{:S(2)}) async-start(), calls=%async_computation.4 | async-start | bytes 13107200 | tf_op jit(solution)/shard_map/all_gather | solution.py:35
  7.9 437.4 %all-gather.5.cloned.1.call-start = ((), (), s32[]{:S(2)}) async-start(), calls=%async_computation.5 | async-start | bytes 13516800 | tf_op jit(solution)/shard_map/all_gather | solution.py:45
  287.4 7.7 %copy-start.2 = (f32[5120,40]{0,1:T(8,128)S(1)}, f32[5120,40]{0,1:T(8,128)}, u32[]{:S(2)}) copy-start(f32[5120,40]{0,1:T(8,128)} %param.9) | copy-start | bytes 2457604
  287.4 7.7 %copy-start.3 = (f32[5120,40]{0,1:T(8,128)S(1)}, f32[5120,40]{0,1:T(8,128)}, u32[]{:S(2)}) copy-start(f32[5120,40]{0,1:T(8,128)} %param.7) | copy-start | bytes 2457604
  299.7 22.6 %all-to-all-start.3 = ((bf16[32,160,40]{1,2,0:T(8,128)(2,1)}), bf16[32,160,40]{1,2,0:T(8,128)(2,1)S(1)}, u32[]{:S(2)}, u32[]{:S(2)}) async-start(bf16[32,160,40]{1,2,0:T(8,128)(2,1)} %copy.28), calls=%async_computation.3 | async-start | bytes 1310720 | tf_op jit(solution)/shard_map/all_to_all | solution.py:53
  322.4 18.1 %all-to-all-start.2 = ((bf16[32,160,40]{1,2,0:T(8,128)(2,1)}), bf16[32,160,40]{1,2,0:T(8,128)(2,1)S(1)}, u32[]{:S(2)}, u32[]{:S(2)}) async-start(bf16[32,160,40]{1,2,0:T(8,128)(2,1)} %copy.27), calls=%async_computation.2 | async-start | bytes 1310720 | tf_op jit(solution)/shard_map/all_to_all | solution.py:50
  340.5 23.1 %all-to-all-start.1 = ((bf16[32,160,40]{1,2,0:T(8,128)(2,1)}), bf16[32,160,40]{1,2,0:T(8,128)(2,1)S(1)}, u32[]{:S(2)}, u32[]{:S(2)}) async-start(bf16[32,160,40]{1,2,0:T(8,128)(2,1)} %copy.26), calls=%async_computation.1 | async-start | bytes 1310720 | tf_op jit(solution)/shard_map/all_to_all | solution.py:47
  364.8 98.1 %copy-start.1 = (bf16[1024,1280]{1,0:T(8,128)(2,1)S(1)}, bf16[1024,1280]{1,0:T(8,128)(2,1)}, u32[]{:S(2)}) copy-start(bf16[1024,1280]{1,0:T(8,128)(2,1)} %param.6) | copy-start | bytes 7864324
Sparse Core Ops, SparseCore 0:
  9.6 99.5 all-gather.2
  297.8 147.3 all-gather.4
where the time goes:
time: 471 us; the launch traced here: 470 us
  waiting for transfers between devices  220 us (47%)
  blocking collectives  158 us (34%)
  local copies, waits for them, and re-layouts  29.9 us (6%)
  matrix products  20.2 us (4%)
  starting transfers between devices  15.8 us (3%)
  between operations  14.1 us (3%)
  other arithmetic  11.6 us (2%)
    all_to_all x1, blocking collectives, sent_and_summed(): parts = lax.all_to_all(split_up(value, dim, count), axis, 0, 0, tiled=True)  158 us
    all_gather x1, waiting for transfers between devices, body(): gathered = lax.all_gather(activations, 'tensor', axis=1, tiled=True)  101 us
    all_gather x1, waiting for transfers between devices, body(): lax.all_gather(weights_old.astype(jnp.bfloat16), 'fsdp', axis=1, tiled=True)  77.8 us
    unnamed x12, local copies, waits for them, and re-layouts  22.9 us
    dot_general x1, matrix products, body(): lax.dot_general(cotangent, gathered, (((0,), (0,)), ((), ())), preferred_...  20.2 us
    all_to_all x1, waiting for transfers between devices, body(): lax.all_to_all(weights_old.astype(jnp.bfloat16), 'fsdp', split_axis=0, co...  16.4 us
    all_to_all x1, waiting for transfers between devices, body(): lax.all_to_all(second_old.astype(jnp.bfloat16), 'fsdp', split_axis=0, con...  13.6 us
    all_to_all x1, waiting for transfers between devices, body(): lax.all_to_all(first_old.astype(jnp.bfloat16), 'fsdp', split_axis=0, conc...  10.4 us
  transfers between devices with their start and end apart: 5, of which 5 were waited for; matrix products, arithmetic and copies ran while one was open for 2% of the time, Pallas kernels for 0%

commit v1 on v0

--- a/solution.py
+++ b/solution.py
@@ -2,6 +2,7 @@
 import jax.numpy as jnp
 from jax import lax
 from jax.sharding import PartitionSpec as P
+from jax.lax import all_gather
 
 STEP = 20
 beta_one = 0.9
@@ -32,7 +33,7 @@
 
 
 def body(activations, cotangent, weights, first_moment, second_moment):
-    gathered = lax.all_gather(activations, "tensor", axis=1, tiled=True)
+    gathered = jnp.concatenate(all_gather(activations, axis_name="tensor"), 1)
     transposed = sent_and_summed(
         lax.dot_general(
             cotangent, gathered, (((0,), (0,)), ((), ())), preferred_element_type=jnp.float32

time: 471 us -> 486 us (1.032)
  local copies, waits for them, and re-layouts: 29.9 us -> 44.3 us
    reshape x0 -> x1, local copies, waits for them, and re-layouts: none -> 14.4 us  [body(): gathered = jnp.concatenate(all_gather(activations, axis_name='tensor'), 1)]
where the time goes in v1:
time: 486 us; the launch traced here: 484 us
  waiting for transfers between devices  217 us (45%)
  blocking collectives  158 us (33%)
  local copies, waits for them, and re-layouts  44.3 us (9%)
  matrix products  20.5 us (4%)
  starting transfers between devices  18.7 us (4%)
  between operations  14.1 us (3%)
  other arithmetic  11.6 us (2%)
    all_to_all x1, blocking collectives, sent_and_summed(): parts = lax.all_to_all(split_up(value, dim, count), axis, 0, 0, tiled=True)  158 us
    all_gather x1, waiting for transfers between devices, body(): gathered = jnp.concatenate(all_gather(activations, axis_name='tensor'), 1)  101 us
    all_gather x1, waiting for transfers between devices, body(): lax.all_gather(weights_old.astype(jnp.bfloat16), 'fsdp', axis=1, tiled=True)  77.6 us
    unnamed x12, local copies, waits for them, and re-layouts  22.9 us
    dot_general x1, matrix products, body(): lax.dot_general(cotangent, gathered, (((0,), (0,)), ((), ())), preferred_...  20.5 us
    all_to_all x1, waiting for transfers between devices, body(): lax.all_to_all(second_old.astype(jnp.bfloat16), 'fsdp', split_axis=0, con...  15.6 us
    reshape x1, local copies, waits for them, and re-layouts, body(): gathered = jnp.concatenate(all_gather(activations, axis_name='tensor'), 1)  14.4 us
    all_to_all x1, waiting for transfers between devices, body(): lax.all_to_all(weights_old.astype(jnp.bfloat16), 'fsdp', split_axis=0, co...  12.3 us
  transfers between devices with their start and end apart: 5, of which 5 were waited for; matrix products, arithmetic and copies ran while one was open for 2% of the time, Pallas kernels for 0%

profile of v1, /device:TPU:0, one launch (start us, length us, event | category | flops | bytes accessed | tf_op | source)
XLA Modules:
  0.0 484.4 jit_solution(18147997051075165703)
XLA Ops:
  8.0 101.3 %all-gather.6.cloned.1.call-done = bf16[4096,1280]{1,0:T(8,128)(2,1)} async-done(((bf16[1024,1280]{1,0:T(8,128)(2,1)}), bf16[4096,1280]{1,0:T(8,128)(2,1)}) %all-gather.6.cloned.1.call-update) | async-done | bytes 10485776 | tf_op jit(solution)/shard_map/all_gather | solution.py:36
  109.3 14.4 %copy.37 = bf16[1024,4,1280]{0,2,1:T(8,128)(2,1)} copy(bf16[1024,4,1280]{2,0,1:T(8,128)(2,1)} %bitcast.36) | data formatting | bytes 20971520 | tf_op jit(solution)/shard_map/reshape | solution.py:36
  123.7 20.5 %convolution_convert_fusion = bf16[1280,5120]{1,0:T(8,128)(2,1)} fusion(bf16[1024,1280]{1,0:T(8,128)(2,1)S(1)} %copy-done, bf16[1024,5120]{0,1:T(8,128)(2,1)} %bitcast.37), kind=kOutput, calls=%fused_computation.1 | convolution fusion | flops 13428326400 | bytes 26214400 | tf_op jit(solution)/shard_map/dot_general | solution.py:38
  144.2 158.0 %all_to_all.44 = bf16[32,40,5120]{2,1,0:T(8,128)(2,1)} all-to-all(bf16[32,40,5120]{2,1,0:T(8,128)(2,1)} %bitcast.35), channel_id=1, replica_groups=mesh['fsdp'=32,'tensor'=4] {'fsdp'}, dimensions={0} | all-to-all | bytes 26214400 | tf_op jit(solution)/shard_map/all_to_all | solution.py:22
  302.2 7.7 %convert_reduce_fusion = f32[40,5120]{1,0:T(8,128)S(1)} fusion(bf16[32,40,5120]{2,1,0:T(8,128)(2,1)} %all_to_all.44), kind=kLoop, calls=%fused_computation | loop fusion | flops 12902400 | bytes 13926400 | tf_op jit(solution)/shard_map/reduce_sum | solution.py:23
  309.8 2.6 fusion.3
  312.4 0.8 all_to_all.38
  313.3 1.2 copy.40
  314.5 10.4 %all-to-all-start.3 = ((bf16[32,160,40]{1,2,0:T(8,128)(2,1)}), bf16[32,160,40]{1,2,0:T(8,128)(2,1)S(1)}, u32[]{:S(2)}, u32[]{:S(2)}) async-start(bf16[32,160,40]{1,2,0:T(8,128)(2,1)} %copy.40), calls=%async_computation.3 | async-start | bytes 1310720 | tf_op jit(solution)/shard_map/all_to_all | solution.py:54
  324.9 0.8 all_to_all.36
  325.7 1.2 copy.39
  326.9 15.6 %all-to-all-done.3 = bf16[32,160,40]{1,2,0:T(8,128)(2,1)S(1)} async-done(((bf16[32,160,40]{1,2,0:T(8,128)(2,1)}), bf16[32,160,40]{1,2,0:T(8,128)(2,1)S(1)}, u32[]{:S(2)}, u32[]{:S(2)}) %all-to-all-start.3) | async-done | bytes 409632 | tf_op jit(solution)/shard_map/all_to_all | solution.py:54
  342.5 4.1 all-to-all-start.2
  346.7 1.8 all_to_all.34
  348.5 1.2 copy.38
  349.7 9.6 %all-to-all-done.2 = bf16[32,160,40]{1,2,0:T(8,128)(2,1)S(1)} async-done(((bf16[32,160,40]{1,2,0:T(8,128)(2,1)}), bf16[32,160,40]{1,2,0:T(8,128)(2,1)S(1)}, u32[]{:S(2)}, u32[]{:S(2)}) %all-to-all-start.2) | async-done | bytes 409632 | tf_op jit(solution)/shard_map/all_to_all | solution.py:51
  359.3 4.1 all-to-all-start.1
  363.5 1.3 copy.43
  364.9 1.3 copy.42
  366.2 12.3 %all-to-all-done.1 = bf16[32,160,40]{1,2,0:T(8,128)(2,1)S(1)} async-done(((bf16[32,160,40]{1,2,0:T(8,128)(2,1)}), bf16[32,160,40]{1,2,0:T(8,128)(2,1)S(1)}, u32[]{:S(2)}, u32[]{:S(2)}) %all-to-all-start.1) | async-done | bytes 409632 | tf_op jit(solution)/shard_map/all_to_all | solution.py:48
  378.5 1.2 convert_element_type.60
  379.6 2.7 copy.41
  382.3 77.6 %all-gather.4.cloned.1.call-done = bf16[5120,1280]{0,1:T(8,128)(2,1)} async-done(((bf16[5120,40]{0,1:T(8,128)(2,1)}), bf16[5120,1280]{0,1:T(8,128)(2,1)}) %all-gather.4.cloned.1.call-update) | async-done | bytes 13107216 | tf_op jit(solution)/shard_map/all_gather | solution.py:46
  460.0 17.6 %copy.44 = bf16[5120,1280]{1,0:T(8,128)(2,1)} copy(bf16[5120,1280]{0,1:T(8,128)(2,1)} %all-gather.4.cloned.1.call-done) | data formatting | bytes 26214400
  (14 shorter events, 1.0 us)
Async XLA Ops:
  7.2 116.5 %copy-start = (bf16[1024,1280]{1,0:T(8,128)(2,1)S(1)}, bf16[1024,1280]{1,0:T(8,128)(2,1)}, u32[]{:S(2)}) copy-start(bf16[1024,1280]{1,0:T(8,128)(2,1)} %param.6) | copy-start | bytes 7864324
  7.2 102.1 %all-gather.6.cloned.1.call-start = ((), (), s32[]{:S(2)}) async-start(), calls=%async_computation.5 | async-start | bytes 13107200 | tf_op jit(solution)/shard_map/all_gather | solution.py:36
  7.9 452.1 %all-gather.4.cloned.1.call-start = ((), (), s32[]{:S(2)}) async-start(), calls=%async_computation.4 | async-start | bytes 13516800 | tf_op jit(solution)/shard_map/all_gather | solution.py:46
  302.2 7.7 %copy-start.2 = (f32[5120,40]{0,1:T(8,128)S(1)}, f32[5120,40]{0,1:T(8,128)}, u32[]{:S(2)}) copy-start(f32[5120,40]{0,1:T(8,128)} %param.9) | copy-start | bytes 2457604
  302.2 7.7 %copy-start.3 = (f32[5120,40]{0,1:T(8,128)S(1)}, f32[5120,40]{0,1:T(8,128)}, u32[]{:S(2)}) copy-start(f32[5120,40]{0,1:T(8,128)} %param.7) | copy-start | bytes 2457604
  314.5 28.0 %all-to-all-start.3 = ((bf16[32,160,40]{1,2,0:T(8,128)(2,1)}), bf16[32,160,40]{1,2,0:T(8,128)(2,1)S(1)}, u32[]{:S(2)}, u32[]{:S(2)}) async-start(bf16[32,160,40]{1,2,0:T(8,128)(2,1)} %copy.40), calls=%async_computation.3 | async-start | bytes 1310720 | tf_op jit(solution)/shard_map/all_to_all | solution.py:54
  342.5 16.8 %all-to-all-start.2 = ((bf16[32,160,40]{1,2,0:T(8,128)(2,1)}), bf16[32,160,40]{1,2,0:T(8,128)(2,1)S(1)}, u32[]{:S(2)}, u32[]{:S(2)}) async-start(bf16[32,160,40]{1,2,0:T(8,128)(2,1)} %copy.39), calls=%async_computation.2 | async-start | bytes 1310720 | tf_op jit(solution)/shard_map/all_to_all | solution.py:51
  359.3 19.2 %all-to-all-start.1 = ((bf16[32,160,40]{1,2,0:T(8,128)(2,1)}), bf16[32,160,40]{1,2,0:T(8,128)(2,1)S(1)}, u32[]{:S(2)}, u32[]{:S(2)}) async-start(bf16[32,160,40]{1,2,0:T(8,128)(2,1)} %copy.38), calls=%async_computation.1 | async-start | bytes 1310720 | tf_op jit(solution)/shard_map/all_to_all | solution.py:48
  379.6 98.0 %copy-start.1 = (bf16[1024,1280]{1,0:T(8,128)(2,1)S(1)}, bf16[1024,1280]{1,0:T(8,128)(2,1)}, u32[]{:S(2)}) copy-start(bf16[1024,1280]{1,0:T(8,128)(2,1)} %param.6) | copy-start | bytes 7864324
Sparse Core Ops, SparseCore 0:
  9.6 99.5 all-gather.5
  312.6 147.3 all-gather.3
